TPU v7x, 128 devices: a whole 4x4x4 slice. The times are simulated.
128 devices in a mesh: slab: 8 (over z, core), tile: 16 (over x, y).
Axes of the slice: x: 4, y: 4, z: 4, core: 2. Of those that a mesh axis runs over, the one named last changes fastest.
Arguments:
- coarse: bfloat16 [192, 32, 64, 64], P(None, 'slab', 'tile'), may hold values from -6 to 6
- up_weight: bfloat16 [3, 3, 96, 192], replicated, may hold values from -0.15625 to 0.15625
- up_bias: float32 [96], replicated, may hold values from -3 to 3
- gain_one: float32 [96], replicated, may hold values from 0.1 to 1.9
- conv_one: bfloat16 [3, 3, 96, 288], replicated, may hold values from -0.125 to 0.125
- bias_one: float32 [96], replicated, may hold values from -3 to 3
- gain_two: float32 [96], replicated, may hold values from 0.1 to 1.9
- conv_two: bfloat16 [3, 3, 96, 288], replicated, may hold values from -0.125 to 0.125
- bias_two: float32 [96], replicated, may hold values from -3 to 3
Outputs:
- decoded: bfloat16 [96, 32, 128, 128], P(None, 'slab', 'tile')
All inputs are finite; a program needn't handle non-finite values.
Results may differ from a plain program's by a relative error of at most 0.009.
Values may be sent and summed in bfloat16 or wider, within the bound.
No kernel may reach another device: no remote copies, remote signals or barrier semaphores. Data moves between devices by JAX's collectives and lax.ppermute only.
A program may use at most 64 MiB of HBM per device.

v0:
```python
import jax
import jax.numpy as jnp
import numpy as np
from jax import lax
from jax.experimental import pallas as pl
from jax.experimental.pallas import tpu as pltpu
from jax.sharding import PartitionSpec as P

F32 = jnp.float32
BF16 = jnp.bfloat16
CH = 96
VMEM = pl.BlockSpec(memory_space=pltpu.VMEM)
SMEM = pl.BlockSpec(memory_space=pltpu.SMEM)
ANY = pl.BlockSpec(memory_space=pl.ANY)
HBM = pl.BlockSpec(memory_space=pltpu.HBM)


def silu(y):
    return y * (0.5 + 0.5 * jnp.tanh(0.5 * y))


def norm_act(v, gain):
    meansq = jnp.sum(v * v, axis=0, keepdims=True) * (1.0 / CH)
    return silu(v * lax.rsqrt(meansq + 1e-06) * gain)


def lanes_of(shape):
    return lax.broadcasted_iota(jnp.int32, shape, 1)


def weave_matrix():
    m = np.zeros((256, 256), np.float32)
    for h in range(2):
        for q in range(2):
            for j in range(64):
                m[h * 128 + q * 64 + j, h * 128 + 2 * j + q] = 1
    return m


def up_tile(top, bottom, p, wup_ref, cols_ref, emit):
    lane = lanes_of((CH, 128))
    dims = (((1,), (1,)), ((), ()))
    u = lax.dot_general(wup_ref[2 * p], top.reshape(256, 192), dims, preferred_element_type=F32)
    u = u + lax.dot_general(wup_ref[2 * p + 1], bottom.reshape(256, 192), dims, preferred_element_type=F32)
    for g in range(2):
        part = u[:, 128 * g:128 * g + 128]
        even = part[:CH] + jnp.where(lane % 64 == 0, 0.0, pltpu.roll(part[CH:2 * CH], 1, 1)) + cols_ref[0]
        odd = part[2 * CH:3 * CH] + jnp.where(lane % 64 == 63, 0.0, pltpu.roll(part[3 * CH:], 127, 1)) + cols_ref[0]
        even, odd = even.astype(BF16).astype(F32), odd.astype(BF16).astype(F32)
        emit(2 * g, jnp.where(lane < 64, even, pltpu.roll(odd, 64, 1)))
        emit(2 * g + 1, jnp.where(lane < 64, pltpu.roll(even, 64, 1), odd))


def conv_pair(src, w_ref, f, r):
    taps = [
        jnp.concatenate([src(f + t, r + a), src(f + t, r + a + 1)], axis=1)
        for t in range(3) for a in range(3)
    ]
    s = jnp.dot(w_ref[...], jnp.concatenate(taps, axis=0), preferred_element_type=F32)
    lane = lanes_of((CH, 128))
    edge = jnp.logical_or(lane == 0, lane == 127)
    rows = []
    for h in range(2):
        part = s[:, 128 * h:128 * h + 128]
        left, right = part[:CH], part[2 * CH:]
        near = pltpu.roll(jnp.where(lane < 64, left, right), 64, 1)
        far = jnp.where(lane < 64, right, left)
        far = jnp.where(lane < 64, pltpu.roll(far, 65, 1), pltpu.roll(far, 63, 1))
        rows.append(part[CH:2 * CH] + near + jnp.where(edge, 0.0, far))
    return rows


def hidden_frame(src, f, w_ref, cols_ref, hid_ref, has_top, has_bottom):
    for pair in range(5):
        rows = conv_pair(src, w_ref, f, 2 * pair)
        for h in range(2):
            q = 2 * pair + h
            act = norm_act(rows[h] + cols_ref[2], cols_ref[3])
            if q == 0:
                act = jnp.where(has_top, act, 0.0)
            if q == 9:
                act = jnp.where(has_bottom, act, 0.0)
            hid_ref[f, q] = act.astype(BF16)


def decoded_frames(src, w_ref, weave_ref, cols_ref, raw, both_ref, mix_ref, res_ref, out_ref, start, sems):
    copies = []

    def finish(f):
        woven = jnp.dot(both_ref[f], weave_ref[...], preferred_element_type=F32)
        for r in range(8):
            at, h = CH * (r // 2), 128 * (r % 2)
            mix_ref[f, pl.ds(r, CH, stride=8), :] = woven[at:at + CH, h:h + 128]
        res_ref[:, f] = mix_ref[f].reshape(CH, 8, 128).astype(BF16)
        copies.append(pltpu.make_async_copy(res_ref.at[:, f], out_ref.at[:, start + f], sems.at[f]))
        copies[f].start()

    for n in range(8):
        f, pair = n // 4, n % 4
        rows = conv_pair(src, w_ref, f, 2 * pair)
        res = [raw(f, 2 * pair + h).astype(F32) + rows[h] + cols_ref[4] for h in range(2)]
        both_ref[f, CH * pair:CH * pair + CH] = jnp.concatenate([v.astype(BF16) for v in res], axis=1)
        if n == 5:
            finish(0)
    finish(1)
    for copy in copies:
        copy.wait()


def prep_kernel(x_ref, up_ref, one_ref, two_ref, upb_ref, g1_ref, b1_ref, g2_ref, b2_ref,
                wup_ref, w1_ref, w2_ref, cols_ref, act_ref, raw_ref, one_buf, two_buf, sems):
    loads = [
        pltpu.make_async_copy(one_ref, one_buf, sems.at[0]),
        pltpu.make_async_copy(two_ref, two_buf, sems.at[1]),
    ]
    for load in loads:
        load.start()
    for n in range(4):
        taps = []
        for b in range(3):
            if n == 0:
                tap = up_ref[0, b].astype(F32)
            elif n == 3:
                tap = up_ref[2, b].astype(F32)
            else:
                tap = up_ref[1, b].astype(F32) + up_ref[2 if n == 1 else 0, b].astype(F32)
            taps.append(tap)
        for m, tap in enumerate((taps[1] + taps[2], taps[0], taps[0] + taps[1], taps[2])):
            wup_ref[n, CH * m:CH * m + CH, :] = tap.astype(BF16)
    for n, ref in enumerate((upb_ref, g1_ref, b1_ref, g2_ref, b2_ref)):
        cols_ref[n] = jnp.broadcast_to(ref[...], (128, CH)).T
    for k in range(3):
        for n, p in enumerate((1, 0)):
            def emit(f, v, to=2 * k + n):
                raw_ref[f, to] = v.astype(BF16)
                act_ref[f, to] = norm_act(v, cols_ref[1]).astype(BF16)

            up_tile(x_ref[:, k], x_ref[:, k + 1], p, wup_ref, cols_ref, emit)
    for load, src_ref, dst_ref in ((loads[0], one_buf, w1_ref), (loads[1], two_buf, w2_ref)):
        load.wait()
        for b in range(3):
            pieces = [src_ref[t, a][:, CH * b:CH * b + CH] for t in range(3) for a in range(3)]
            dst_ref[CH * b:CH * b + CH, :] = jnp.concatenate(pieces, axis=1)


def first_kernel(flags, x_ref, above_ref, below_ref, wup_ref, w1_ref, cols_ref, inner_ref,
                 act_ref, edge_ref, hid_ref):
    has_top, has_bottom = flags[0] > 0, flags[1] > 0
    act_ref[:, 3:9] = inner_ref[...]
    above, below = above_ref[...], below_ref[...]
    above, below = (above[..., :192], above[..., 192:]), (below[..., :192], below[..., 192:])
    tiles = (
        (0, above[0], above[1], 0, has_top, None),
        (1, above[1], x_ref[:, 0], 1, has_top, None),
        (2, above[1], x_ref[:, 0], 0, None, 0),
        (9, x_ref[:, 3], below[0], 1, None, 1),
        (10, x_ref[:, 3], below[0], 0, has_bottom, None),
        (11, below[0], below[1], 1, has_bottom, None),
    )
    for r, top, bottom, p, ok, keep in tiles:
        def emit(f, v, r=r, ok=ok, keep=keep):
            if keep is not None:
                edge_ref[f, keep] = v.astype(BF16)
            act = norm_act(v, cols_ref[1])
            if ok is not None:
                act = jnp.where(ok, act, 0.0)
            act_ref[f, r] = act.astype(BF16)

        up_tile(top, bottom, p, wup_ref, cols_ref, emit)
    for f in range(2):
        hidden_frame(lambda i, r: act_ref[i, r], f, w1_ref, cols_ref, hid_ref, has_top, has_bottom)


def raw_rows(inner_ref, edge_ref, first):
    def load(f, r):
        if r in (0, 7):
            return edge_ref[first + f, r // 7]
        return inner_ref[first + f, r - 1]

    return load


def second_kernel(flags, old_ref, wup_ref, weave_ref, w1_ref, w2_ref, cols_ref, act_ref, inner_ref, edge_ref, new_ref,
                  hid_ref, out_ref, past_act_ref, rows_ref, both_ref, mix_ref, res_ref, sems):
    has_top, has_bottom, has_old = flags[0] > 0, flags[1] > 0, flags[2] > 0
    for k in range(4):
        both = old_ref[:, k]
        rows_ref[:, 2 * k] = both[..., :192]
        rows_ref[:, 2 * k + 1] = both[..., 192:]
    for i in range(0, 6, 2):
        for p in range(2):
            def emit(n, v, i=i, p=p):
                at = i + n % 2
                ok = has_old
                if at == 0:
                    ok = jnp.logical_and(ok, has_top)
                if at == 5:
                    ok = jnp.logical_and(ok, has_bottom)
                past_act_ref[n // 2, 2 * at + p] = jnp.where(ok, norm_act(v, cols_ref[1]), 0.0).astype(BF16)

            up_tile(rows_ref[:, i + p:i + p + 2], rows_ref[:, i + p + 1:i + p + 3], p, wup_ref, cols_ref, emit)

    def act(f, r):
        return past_act_ref[f, r] if f < 2 else act_ref[f - 2, r]

    def hid(f, r):
        return hid_ref[f, r] if f < 2 else new_ref[f - 2, r]

    for f in range(2):
        hidden_frame(act, f, w1_ref, cols_ref, hid_ref, has_top, has_bottom)
    decoded_frames(hid, w2_ref, weave_ref, cols_ref, raw_rows(inner_ref, edge_ref, 2), both_ref, mix_ref, res_ref, out_ref, 2,
                   sems)


def third_kernel(w2_ref, weave_ref, cols_ref, inner_ref, edge_ref, past_ref, hid_ref, _, out_ref, both_ref, mix_ref, res_ref, sems):
    def hid(f, r):
        return past_ref[f, r] if f < 2 else hid_ref[f - 2, r]

    decoded_frames(hid, w2_ref, weave_ref, cols_ref, raw_rows(inner_ref, edge_ref, 0), both_ref, mix_ref, res_ref, out_ref, 0,
                   sems)


def shape(*dims, dtype=BF16):
    return jax.ShapeDtypeStruct(dims, dtype)


def call(kernel, name, flops, in_specs, out_shape, out_specs, scratch=(), **kw):
    return pl.pallas_call(
        kernel,
        out_shape=out_shape,
        in_specs=in_specs,
        out_specs=out_specs,
        scratch_shapes=list(scratch),
        compiler_params=pltpu.CompilerParams(vmem_limit_bytes=48 << 20),
        cost_estimate=pl.CostEstimate(flops=flops, transcendentals=0, bytes_accessed=4 << 20),
        name=name,
        **kw,
    )


def shards(coarse, up_weight, up_bias, gain_one, conv_one, bias_one, gain_two, conv_two, bias_two):
    tiles, slabs = lax.axis_size("tile"), lax.axis_size("slab")
    later = [(i, i + 1) for i in range(slabs - 1)]
    x = coarse.transpose(1, 2, 3, 0)
    low, high = (jnp.concatenate([x[:, i], x[:, i + 1]], axis=2) for i in (0, 2))
    above = lax.ppermute(high, "tile", [(i, i + 1) for i in range(tiles - 1)])
    below = lax.ppermute(low, "tile", [(i + 1, i) for i in range(tiles - 1)])
    wup, w1, w2, cols, inner_act, inner_raw = call(
        prep_kernel, "prep", 2 << 30, [VMEM, VMEM, HBM, HBM] + [VMEM] * 5,
        (shape(4, 4 * CH, 192), shape(3 * CH, 9 * CH), shape(3 * CH, 9 * CH), shape(5, CH, 128, dtype=F32),
         shape(4, 6, CH, 128), shape(4, 6, CH, 128)), (VMEM,) * 6,
        [pltpu.VMEM((3, 3, CH, 3 * CH), BF16), pltpu.VMEM((3, 3, CH, 3 * CH), BF16), pltpu.SemaphoreType.DMA((2,))],
    )(x, up_weight, conv_one, conv_two, *(v.reshape(1, CH) for v in (up_bias, gain_one, bias_one, gain_two, bias_two)))
    weave = jnp.asarray(weave_matrix(), BF16)
    place, age = lax.axis_index("tile"), lax.axis_index("slab")
    flags = jnp.stack([place, tiles - 1 - place, age]).astype(jnp.int32)
    old = lax.ppermute(jnp.stack([above[2:], low[2:], high[2:], below[2:]], axis=1), "slab", later)
    act, edge_raw, new = call(
        first_kernel, "first", 3 << 30, [SMEM] + [VMEM] * 7,
        (shape(4, 12, CH, 128), shape(4, 2, CH, 128), shape(2, 10, CH, 128)), (VMEM,) * 3,
    )(flags, x, above, below, wup, w1, cols, inner_act)
    past = lax.ppermute(new, "slab", later)
    results = [pltpu.VMEM((2, 4 * CH, 256), BF16), pltpu.VMEM((2, CH * 8, 128), F32), pltpu.VMEM((CH, 2, 8, 128), BF16), pltpu.SemaphoreType.DMA((2,))]
    hid, out = call(
        second_kernel, "second", 3 << 30, [SMEM] + [VMEM] * 10,
        (shape(2, 10, CH, 128), shape(CH, 4, 8, 128)), (VMEM, ANY),
        [pltpu.VMEM((2, 12, CH, 128), BF16), pltpu.VMEM((2, 8, 64, 192), BF16)] + results,
    )(flags, old, wup, weave, w1, w2, cols, act, inner_raw, edge_raw, new)
    return call(
        third_kernel, "third", 1 << 30, [VMEM] * 7 + [ANY],
        shape(CH, 4, 8, 128), ANY, results, input_output_aliases={7: 0},
    )(w2, weave, cols, inner_raw, edge_raw, past, hid, out)


def solution(mesh):
    return jax.shard_map(
        shards,
        mesh=mesh,
        in_specs=(P(None, "slab", "tile", None), P(), P(), P(), P(), P(), P(), P(), P()),
        out_specs=P(None, "slab", "tile", None),
        check_vma=False,
    )
```

profile of v0, /device:TPU:56, one launch (start us, length us, event | category | flops | bytes accessed | tf_op | source)
XLA Modules:
  0.0 33.3 jit_solution(1062161494893703502)
XLA Ops:
  0.0 1.1 %copy.20 = bf16[192,4,4,64]{0,3,1,2:T(8,128)(2,1)S(1)} copy(bf16[192,4,4,64]{0,3,2,1:T(8,128)(2,1)} %param.10) | data formatting | bytes 786432 | tf_op args[0]
  1.1 0.0 copy-start
  1.1 0.0 copy-start.2
  1.1 0.0 copy-start.3
  1.1 0.0 copy-start.4
  1.1 0.0 copy-start.5
  1.1 0.0 copy-start.6
  1.2 0.0 copy-start.7
  1.2 0.0 copy-start.8
  1.2 0.0 copy-start.9
  1.2 0.1 pad_maximum_fusion.1
  1.4 3.2 %collective-permute-start = (bf16[4,64,384]{2,1,0:T(8,128)(2,1)S(1)}, bf16[4,64,384]{2,1,0:T(8,128)(2,1)S(1)}, u32[]{:S(2)}, u32[]{:S(2)}) collective-permute-start(bf16[4,64,384]{2,1,0:T(8,128)(2,1)S(1)} %pad_maximum_fusion.1), channel_id=1, source_target_pairs={{0,1},{1,2},{2,3},{3,4},{4,5},{5,6},{6,7},{7,8},{8,9},{9,10},{10,1... | collective-permute-start | bytes 589832 | tf_op jit(solution)/shard_map/ppermute | solution.py:246
  4.5 0.1 pad_maximum_fusion.2
  4.7 2.8 %collective-permute-start.1 = (bf16[4,64,384]{2,1,0:T(8,128)(2,1)S(1)}, bf16[4,64,384]{2,1,0:T(8,128)(2,1)S(1)}, u32[]{:S(2)}, u32[]{:S(2)}) collective-permute-start(bf16[4,64,384]{2,1,0:T(8,128)(2,1)S(1)} %pad_maximum_fusion.2), channel_id=1, source_target_pairs={{1,0},{2,1},{3,2},{4,3},{5,4},{6,5},{7,6},{8,7},{9,8},{10,9},{11,1... | collective-permute-start | bytes 589832 | tf_op jit(solution)/shard_map/ppermute | solution.py:247
  7.5 0.1 fusion.1
  7.6 0.1 pad_add_fusion.flags
  7.6 0.0 copy-done
  7.7 0.0 copy-done.2
  7.7 0.0 copy-done.3
  7.7 2.3 %prep.1 = (bf16[4,384,192]{2,1,0:T(8,128)(2,1)S(1)}, bf16[288,864]{1,0:T(8,128)(2,1)S(1)}, bf16[288,864]{1,0:T(8,128)(2,1)S(1)}, f32[5,96,128]{2,1,0:T(8,128)S(1...) custom-call(bf16[4,4,64,192]{3,2,1,0:T(8,128)(2,1)S(1)} %bitcast.34, ...), custom_call_target="tpu_custom_call" | custom-call | flops 2147483648 | bytes 4194304 | tf_op jit(solution)/shard_map/prep/pallas_call | solution.py:248
  10.1 0.0 collective-permute-done.above_ref
  10.1 4.9 %collective-permute-done.1.below_ref = bf16[4,64,384]{2,1,0:T(8,128)(2,1)S(1)} collective-permute-done((bf16[4,64,384]{2,1,0:T(8,128)(2,1)S(1)}, bf16[4,64,384]{2,1,0:T(8,128)(2,1)S(1)}, u32[]{:S(2)}, u32[]{:S(2)}) %collective-permute-start.1) | collective-permute-done | bytes 196640 | tf_op jit(solution)/shard_map/ppermute | solution.py:247
  15.0 0.1 pad_maximum_fusion
  15.1 1.9 %collective-permute-start.3 = (bf16[2,4,64,384]{3,2,1,0:T(8,128)(2,1)S(1)}, bf16[2,4,64,384]{3,2,1,0:T(8,128)(2,1)S(1)}, u32[]{:S(2)}, u32[]{:S(2)}) collective-permute-start(bf16[2,4,64,384]{3,2,1,0:T(8,128)(2,1)S(1)} %pad_maximum_fusion), channel_id=1, source_target_pairs={{0,16},{16,32},{32,48},{48,64},{64,80},{80,96},{96,112},{1,17},{17... | collective-permute-start | bytes 1179656 | tf_op jit(solution)/shard_map/ppermute | solution.py:257
  17.0 0.0 copy-start.1
  17.1 3.6 %first.1 = (bf16[4,12,96,128]{3,2,1,0:T(8,128)(2,1)S(1)}, bf16[4,2,96,128]{3,2,1,0:T(8,128)(2,1)S(1)}, bf16[2,10,96,128]{3,2,1,0:T(8,128)(2,1)S(1)}) custom-call(s32[3]{0:T(128)S(1)} %pad_add_fusion.flags, bf16[4,4,64,192]{3,2,1,0:T(8,128)(2,1)S(1)} %bitcast.35, bf16[4,64,384]{2,1,0:T(8,128)(2,1)S(1)} %collective-permute-done.above_ref, ...), custom_call_target="tpu_custom_call" | custom-call | flops 3221225472 | bytes 4194304 | tf_op jit(solution)/shard_map/first/pallas_call | solution.py:258
  20.7 3.9 %collective-permute-start.2 = (bf16[2,10,96,128]{3,2,1,0:T(8,128)(2,1)S(1)}, bf16[2,10,96,128]{3,2,1,0:T(8,128)(2,1)S(1)}, u32[]{:S(2)}, u32[]{:S(2)}) collective-permute-start(bf16[2,10,96,128]{3,2,1,0:T(8,128)(2,1)S(1)} %get-tuple-element.23.new_ref), channel_id=1, source_target_pairs={{0,16},{16,32},{32,48},{48,64},{64,80},{80,96},{96,112},{1,17},{17... | collective-permute-start | bytes 1474568 | tf_op jit(solution)/shard_map/ppermute | solution.py:262
  24.6 0.0 collective-permute-done.3.old_ref
  24.6 0.0 copy-done.1
  24.6 5.8 %second.1 = (bf16[2,10,96,128]{3,2,1,0:T(8,128)(2,1)S(1)}, bf16[96,4,8,128]{3,2,1,0:T(8,128)(2,1)}) custom-call(s32[3]{0:T(128)S(1)} %pad_add_fusion.flags, bf16[2,4,64,384]{3,2,1,0:T(8,128)(2,1)S(1)} %collective-permute-done.3.old_ref, bf16[4,384,192]{2,1,0:T(8,128)(2,1)S(1)} %get-tuple-element.19.wup_ref, bf16[256,256]{1,0:T(8,128)(2,1)S(1)} %copy-done.1, ...), custom_call_target="tpu_custom_call" | custom-call | flops 3221225472 | bytes 4194304 | tf_op jit(solution)/shard_map/second/pallas_call | solution.py:264
  30.5 0.4 %collective-permute-done.2.past_ref = bf16[2,10,96,128]{3,2,1,0:T(8,128)(2,1)S(1)} collective-permute-done((bf16[2,10,96,128]{3,2,1,0:T(8,128)(2,1)S(1)}, bf16[2,10,96,128]{3,2,1,0:T(8,128)(2,1)S(1)}, u32[]{:S(2)}, u32[]{:S(2)}) %collective-permute-start.2) | collective-permute-done | bytes 491552 | tf_op jit(solution)/shard_map/ppermute | solution.py:262
  30.8 2.5 %third.1 = bf16[96,4,8,128]{3,2,1,0:T(8,128)(2,1)} custom-call(bf16[288,864]{1,0:T(8,128)(2,1)S(1)} %get-tuple-element.16.w2_ref, bf16[256,256]{1,0:T(8,128)(2,1)S(1)} %copy-done.1, f32[5,96,128]{2,1,0:T(8,128)S(1)} %get-tuple-element.17.cols_ref, bf16[4,6,96,128]{3,2,1,0:T(8,128)(2,1)S(1)} %get-tuple-element.18.inner_ref, ...), custom_call_target="tpu_custom_call", output_to_operand_aliasing={{}: (7, {})} | custom-call | flops 1073741824 | bytes 4194304 | tf_op jit(solution)/shard_map/third/pallas_call | solution.py:269
  (9 shorter events, 0.1 us)
Async XLA Ops:
  1.1 6.6 %copy-start = (bf16[192,4,4,64]{0,3,2,1:T(8,128)(2,1)S(1)}, bf16[192,4,4,64]{0,3,2,1:T(8,128)(2,1)}, u32[]{:S(2)}) copy-start(bf16[192,4,4,64]{0,3,2,1:T(8,128)(2,1)} %param.10) | copy-start | bytes 1179652
  1.1 6.6 %copy-start.2 = (bf16[3,3,96,288]{3,2,1,0:T(8,128)(2,1)S(1)}, bf16[3,3,96,288]{3,2,1,0:T(8,128)(2,1)}, u32[]{:S(2)}) copy-start(bf16[3,3,96,288]{3,2,1,0:T(8,128)(2,1)} %one_ref.1) | copy-start | bytes 1492996
  1.1 6.6 %copy-start.3 = (bf16[3,3,96,288]{3,2,1,0:T(8,128)(2,1)S(1)}, bf16[3,3,96,288]{3,2,1,0:T(8,128)(2,1)}, u32[]{:S(2)}) copy-start(bf16[3,3,96,288]{3,2,1,0:T(8,128)(2,1)} %two_ref.1) | copy-start | bytes 1492996
  1.1 6.5 %copy-start.4 = (bf16[3,3,96,192]{3,2,1,0:T(8,128)(2,1)S(1)}, bf16[3,3,96,192]{3,2,1,0:T(8,128)(2,1)}, u32[]{:S(2)}) copy-start(bf16[3,3,96,192]{3,2,1,0:T(8,128)(2,1)} %up_ref.1) | copy-start | bytes 995332
  1.1 6.5 %copy-start.5 = (f32[96]{0:T(128)S(1)}, f32[96]{0:T(128)}, u32[]{:S(2)}) copy-start(f32[96]{0:T(128)} %param.12) | copy-start | bytes 1156
  1.1 6.5 %copy-start.6 = (f32[96]{0:T(128)S(1)}, f32[96]{0:T(128)}, u32[]{:S(2)}) copy-start(f32[96]{0:T(128)} %param.13) | copy-start | bytes 1156
  1.2 6.5 %copy-start.7 = (f32[96]{0:T(128)S(1)}, f32[96]{0:T(128)}, u32[]{:S(2)}) copy-start(f32[96]{0:T(128)} %param.15) | copy-start | bytes 1156
  1.2 6.5 %copy-start.8 = (f32[96]{0:T(128)S(1)}, f32[96]{0:T(128)}, u32[]{:S(2)}) copy-start(f32[96]{0:T(128)} %param.16) | copy-start | bytes 1156
  1.2 6.5 %copy-start.9 = (f32[96]{0:T(128)S(1)}, f32[96]{0:T(128)}, u32[]{:S(2)}) copy-start(f32[96]{0:T(128)} %param.18) | copy-start | bytes 1156
  1.4 8.7 %collective-permute-start = (bf16[4,64,384]{2,1,0:T(8,128)(2,1)S(1)}, bf16[4,64,384]{2,1,0:T(8,128)(2,1)S(1)}, u32[]{:S(2)}, u32[]{:S(2)}) collective-permute-start(bf16[4,64,384]{2,1,0:T(8,128)(2,1)S(1)} %pad_maximum_fusion.1), channel_id=1, source_target_pairs={{0,1},{1,2},{2,3},{3,4},{4,5},{5,6},{6,7},{7,8},{8,9},{9,10},{10,1... | collective-permute-start | bytes 589832 | tf_op jit(solution)/shard_map/ppermute | solution.py:246
  4.7 10.4 %collective-permute-start.1 = (bf16[4,64,384]{2,1,0:T(8,128)(2,1)S(1)}, bf16[4,64,384]{2,1,0:T(8,128)(2,1)S(1)}, u32[]{:S(2)}, u32[]{:S(2)}) collective-permute-start(bf16[4,64,384]{2,1,0:T(8,128)(2,1)S(1)} %pad_maximum_fusion.2), channel_id=1, source_target_pairs={{1,0},{2,1},{3,2},{4,3},{5,4},{6,5},{7,6},{8,7},{9,8},{10,9},{11,1... | collective-permute-start | bytes 589832 | tf_op jit(solution)/shard_map/ppermute | solution.py:247
  15.1 9.5 %collective-permute-start.3 = (bf16[2,4,64,384]{3,2,1,0:T(8,128)(2,1)S(1)}, bf16[2,4,64,384]{3,2,1,0:T(8,128)(2,1)S(1)}, u32[]{:S(2)}, u32[]{:S(2)}) collective-permute-start(bf16[2,4,64,384]{3,2,1,0:T(8,128)(2,1)S(1)} %pad_maximum_fusion), channel_id=1, source_target_pairs={{0,16},{16,32},{32,48},{48,64},{64,80},{80,96},{96,112},{1,17},{17... | collective-permute-start | bytes 1179656 | tf_op jit(solution)/shard_map/ppermute | solution.py:257
  17.0 7.6 %copy-start.1 = (bf16[256,256]{1,0:T(8,128)(2,1)S(1)}, bf16[256,256]{1,0:T(8,128)(2,1)}, u32[]{:S(2)}) copy-start(bf16[256,256]{1,0:T(8,128)(2,1)} %constant.13.clone.weave_ref) | copy-start | bytes 393220
  20.7 10.1 %collective-permute-start.2 = (bf16[2,10,96,128]{3,2,1,0:T(8,128)(2,1)S(1)}, bf16[2,10,96,128]{3,2,1,0:T(8,128)(2,1)S(1)}, u32[]{:S(2)}, u32[]{:S(2)}) collective-permute-start(bf16[2,10,96,128]{3,2,1,0:T(8,128)(2,1)S(1)} %get-tuple-element.23.new_ref), channel_id=1, source_target_pairs={{0,16},{16,32},{32,48},{48,64},{64,80},{80,96},{96,112},{1,17},{17... | collective-permute-start | bytes 1474568 | tf_op jit(solution)/shard_map/ppermute | solution.py:262
where the time goes:
time: 33.6 us; the launch traced here: 33.3 us
  Pallas kernels  14.3 us (43%)
  starting transfers between devices  11.8 us (35%)
  waiting for transfers between devices  5.31 us (16%)
  local copies, waits for them, and re-layouts  1.2 us (4%)
  other arithmetic  0.46 us (1%)
    pallas_call x1, Pallas kernels, shards(): call(second_kernel, 'second', 3 << 30, [SMEM] + [VMEM] * 10, (shape(2, 10...  5.82 us
    ppermute x1, waiting for transfers between devices, shards(): below = lax.ppermute(low, 'tile', [(i + 1, i) for i in range(tiles - 1)])  4.94 us
    ppermute x1, starting transfers between devices, shards(): past = lax.ppermute(new, 'slab', later)  3.93 us
    pallas_call x1, Pallas kernels, shards(): call(first_kernel, 'first', 3 << 30, [SMEM] + [VMEM] * 7, (shape(4, 12, C...  3.61 us
    ppermute x1, starting transfers between devices, shards(): above = lax.ppermute(high, 'tile', [(i, i + 1) for i in range(tiles - 1)])  3.19 us
    ppermute x1, starting transfers between devices, shards(): below = lax.ppermute(low, 'tile', [(i + 1, i) for i in range(tiles - 1)])  2.78 us
    pallas_call x1, Pallas kernels, shards(): call(third_kernel, 'third', 1 << 30, [VMEM] * 7 + [ANY], shape(CH, 4, 8,...  2.52 us
    pallas_call x1, Pallas kernels, shards(): call(prep_kernel, 'prep', 2 << 30, [VMEM, VMEM, HBM, HBM] + [VMEM] * 5, (...  2.32 us
  transfers between devices with their start and end apart: 4, of which 2 were waited for; matrix products, arithmetic and copies ran while one was open for 1% of the time, Pallas kernels for 35%

commit v1 on v0

--- a/solution.py
+++ b/solution.py
@@ -51,17 +51,17 @@
         emit(2 * g + 1, jnp.where(lane < 64, pltpu.roll(even, 64, 1), odd))
 
 
-def conv_pair(src, w_ref, f, r):
+def conv_pair(src, w_ref, f, r, s):
     taps = [
-        jnp.concatenate([src(f + t, r + a), src(f + t, r + a + 1)], axis=1)
+        jnp.concatenate([src(f + t, r + a), src(f + t, s + a)], axis=1)
         for t in range(3) for a in range(3)
     ]
-    s = jnp.dot(w_ref[...], jnp.concatenate(taps, axis=0), preferred_element_type=F32)
+    sums = jnp.dot(w_ref[...], jnp.concatenate(taps, axis=0), preferred_element_type=F32)
     lane = lanes_of((CH, 128))
     edge = jnp.logical_or(lane == 0, lane == 127)
     rows = []
     for h in range(2):
-        part = s[:, 128 * h:128 * h + 128]
+        part = sums[:, 128 * h:128 * h + 128]
         left, right = part[:CH], part[2 * CH:]
         near = pltpu.roll(jnp.where(lane < 64, left, right), 64, 1)
         far = jnp.where(lane < 64, right, left)
@@ -70,45 +70,39 @@
     return rows
 
 
-def hidden_frame(src, f, w_ref, cols_ref, hid_ref, has_top, has_bottom):
-    for pair in range(5):
-        rows = conv_pair(src, w_ref, f, 2 * pair)
-        for h in range(2):
-            q = 2 * pair + h
-            act = norm_act(rows[h] + cols_ref[2], cols_ref[3])
-            if q == 0:
+def hidden_frame(src, f, pairs, w_ref, cols_ref, hid_ref, has_top, has_bottom):
+    for pair in pairs:
+        rows = conv_pair(src, w_ref, f, *pair)
+        for q, row in zip(pair, rows):
+            act = norm_act(row + cols_ref[2], cols_ref[3])
+            if q == 0 and has_top is not None:
                 act = jnp.where(has_top, act, 0.0)
-            if q == 9:
+            if q == 9 and has_bottom is not None:
                 act = jnp.where(has_bottom, act, 0.0)
             hid_ref[f, q] = act.astype(BF16)
 
 
-def decoded_frames(src, w_ref, weave_ref, cols_ref, raw, both_ref, mix_ref, res_ref, out_ref, start, sems):
-    copies = []
-
+def decoded_frames(src, w_ref, weave_ref, cols_ref, raw, both_ref, mix_ref, res_ref, done):
     def finish(f):
         woven = jnp.dot(both_ref[f], weave_ref[...], preferred_element_type=F32)
         for r in range(8):
             at, h = CH * (r // 2), 128 * (r % 2)
             mix_ref[f, pl.ds(r, CH, stride=8), :] = woven[at:at + CH, h:h + 128]
         res_ref[:, f] = mix_ref[f].reshape(CH, 8, 128).astype(BF16)
-        copies.append(pltpu.make_async_copy(res_ref.at[:, f], out_ref.at[:, start + f], sems.at[f]))
-        copies[f].start()
+        done(f)
 
     for n in range(8):
         f, pair = n // 4, n % 4
-        rows = conv_pair(src, w_ref, f, 2 * pair)
+        rows = conv_pair(src, w_ref, f, 2 * pair, 2 * pair + 1)
         res = [raw(f, 2 * pair + h).astype(F32) + rows[h] + cols_ref[4] for h in range(2)]
         both_ref[f, CH * pair:CH * pair + CH] = jnp.concatenate([v.astype(BF16) for v in res], axis=1)
         if n == 5:
             finish(0)
     finish(1)
-    for copy in copies:
-        copy.wait()
 
 
 def prep_kernel(x_ref, up_ref, one_ref, two_ref, upb_ref, g1_ref, b1_ref, g2_ref, b2_ref,
-                wup_ref, w1_ref, w2_ref, cols_ref, act_ref, raw_ref, one_buf, two_buf, sems):
+                wup_ref, w1_ref, w2_ref, cols_ref, act_ref, raw_ref, hid_ref, one_buf, two_buf, sems):
     loads = [
         pltpu.make_async_copy(one_ref, one_buf, sems.at[0]),
         pltpu.make_async_copy(two_ref, two_buf, sems.at[1]),
@@ -141,12 +135,15 @@
         for b in range(3):
             pieces = [src_ref[t, a][:, CH * b:CH * b + CH] for t in range(3) for a in range(3)]
             dst_ref[CH * b:CH * b + CH, :] = jnp.concatenate(pieces, axis=1)
-
-
-def first_kernel(flags, x_ref, above_ref, below_ref, wup_ref, w1_ref, cols_ref, inner_ref,
+    for f in range(2):
+        hidden_frame(lambda i, r: act_ref[i, r], f, ((0, 1), (2, 3)), w1_ref, cols_ref, hid_ref, None, None)
+
+
+def first_kernel(flags, x_ref, above_ref, below_ref, wup_ref, w1_ref, cols_ref, inner_ref, inner_hid_ref,
                  act_ref, edge_ref, hid_ref):
     has_top, has_bottom = flags[0] > 0, flags[1] > 0
     act_ref[:, 3:9] = inner_ref[...]
+    hid_ref[:, 3:7] = inner_hid_ref[...]
     above, below = above_ref[...], below_ref[...]
     above, below = (above[..., :192], above[..., 192:]), (below[..., :192], below[..., 192:])
     tiles = (
@@ -168,7 +165,8 @@
 
         up_tile(top, bottom, p, wup_ref, cols_ref, emit)
     for f in range(2):
-        hidden_frame(lambda i, r: act_ref[i, r], f, w1_ref, cols_ref, hid_ref, has_top, has_bottom)
+        hidden_frame(lambda i, r: act_ref[i, r], f, ((0, 1), (2, 7), (8, 9)), w1_ref, cols_ref, hid_ref, has_top,
+                     has_bottom)
 
 
 def raw_rows(inner_ref, edge_ref, first):
@@ -181,7 +179,7 @@
 
 
 def second_kernel(flags, old_ref, wup_ref, weave_ref, w1_ref, w2_ref, cols_ref, act_ref, inner_ref, edge_ref, new_ref,
-                  hid_ref, out_ref, past_act_ref, rows_ref, both_ref, mix_ref, res_ref, sems):
+                  hid_ref, res_ref, past_act_ref, rows_ref, both_ref, mix_ref):
     has_top, has_bottom, has_old = flags[0] > 0, flags[1] > 0, flags[2] > 0
     for k in range(4):
         both = old_ref[:, k]
@@ -207,17 +205,26 @@
         return hid_ref[f, r] if f < 2 else new_ref[f - 2, r]
 
     for f in range(2):
-        hidden_frame(act, f, w1_ref, cols_ref, hid_ref, has_top, has_bottom)
-    decoded_frames(hid, w2_ref, weave_ref, cols_ref, raw_rows(inner_ref, edge_ref, 2), both_ref, mix_ref, res_ref, out_ref, 2,
-                   sems)
-
-
-def third_kernel(w2_ref, weave_ref, cols_ref, inner_ref, edge_ref, past_ref, hid_ref, _, out_ref, both_ref, mix_ref, res_ref, sems):
+        hidden_frame(act, f, [(r, r + 1) for r in range(0, 10, 2)], w1_ref, cols_ref, hid_ref, has_top, has_bottom)
+    decoded_frames(hid, w2_ref, weave_ref, cols_ref, raw_rows(inner_ref, edge_ref, 2), both_ref, mix_ref, res_ref,
+                   lambda f: None)
+
+
+def third_kernel(w2_ref, weave_ref, cols_ref, inner_ref, edge_ref, past_ref, hid_ref, later_ref, out_ref,
+                 both_ref, mix_ref, res_ref, sems):
+    copies = [pltpu.make_async_copy(later_ref, out_ref.at[:, 2:4], sems.at[2])]
+    copies[0].start()
+
     def hid(f, r):
         return past_ref[f, r] if f < 2 else hid_ref[f - 2, r]
 
-    decoded_frames(hid, w2_ref, weave_ref, cols_ref, raw_rows(inner_ref, edge_ref, 0), both_ref, mix_ref, res_ref, out_ref, 0,
-                   sems)
+    def done(f):
+        copies.append(pltpu.make_async_copy(res_ref.at[:, f], out_ref.at[:, f], sems.at[f]))
+        copies[-1].start()
+
+    decoded_frames(hid, w2_ref, weave_ref, cols_ref, raw_rows(inner_ref, edge_ref, 0), both_ref, mix_ref, res_ref, done)
+    for copy in copies:
+        copy.wait()
 
 
 def shape(*dims, dtype=BF16):
@@ -240,36 +247,36 @@
 
 def shards(coarse, up_weight, up_bias, gain_one, conv_one, bias_one, gain_two, conv_two, bias_two):
     tiles, slabs = lax.axis_size("tile"), lax.axis_size("slab")
-    later = [(i, i + 1) for i in range(slabs - 1)]
+    onward = [(i, i + 1) for i in range(slabs - 1)]
     x = coarse.transpose(1, 2, 3, 0)
     low, high = (jnp.concatenate([x[:, i], x[:, i + 1]], axis=2) for i in (0, 2))
     above = lax.ppermute(high, "tile", [(i, i + 1) for i in range(tiles - 1)])
     below = lax.ppermute(low, "tile", [(i + 1, i) for i in range(tiles - 1)])
-    wup, w1, w2, cols, inner_act, inner_raw = call(
+    wup, w1, w2, cols, inner_act, inner_raw, inner_hid = call(
         prep_kernel, "prep", 2 << 30, [VMEM, VMEM, HBM, HBM] + [VMEM] * 5,
         (shape(4, 4 * CH, 192), shape(3 * CH, 9 * CH), shape(3 * CH, 9 * CH), shape(5, CH, 128, dtype=F32),
-         shape(4, 6, CH, 128), shape(4, 6, CH, 128)), (VMEM,) * 6,
+         shape(4, 6, CH, 128), shape(4, 6, CH, 128), shape(2, 4, CH, 128)), (VMEM,) * 7,
         [pltpu.VMEM((3, 3, CH, 3 * CH), BF16), pltpu.VMEM((3, 3, CH, 3 * CH), BF16), pltpu.SemaphoreType.DMA((2,))],
     )(x, up_weight, conv_one, conv_two, *(v.reshape(1, CH) for v in (up_bias, gain_one, bias_one, gain_two, bias_two)))
     weave = jnp.asarray(weave_matrix(), BF16)
     place, age = lax.axis_index("tile"), lax.axis_index("slab")
     flags = jnp.stack([place, tiles - 1 - place, age]).astype(jnp.int32)
-    old = lax.ppermute(jnp.stack([above[2:], low[2:], high[2:], below[2:]], axis=1), "slab", later)
+    old = lax.ppermute(jnp.stack([above[2:], low[2:], high[2:], below[2:]], axis=1), "slab", onward)
     act, edge_raw, new = call(
-        first_kernel, "first", 3 << 30, [SMEM] + [VMEM] * 7,
+        first_kernel, "first", 3 << 30, [SMEM] + [VMEM] * 8,
         (shape(4, 12, CH, 128), shape(4, 2, CH, 128), shape(2, 10, CH, 128)), (VMEM,) * 3,
-    )(flags, x, above, below, wup, w1, cols, inner_act)
-    past = lax.ppermute(new, "slab", later)
-    results = [pltpu.VMEM((2, 4 * CH, 256), BF16), pltpu.VMEM((2, CH * 8, 128), F32), pltpu.VMEM((CH, 2, 8, 128), BF16), pltpu.SemaphoreType.DMA((2,))]
-    hid, out = call(
+    )(flags, x, above, below, wup, w1, cols, inner_act, inner_hid)
+    past = lax.ppermute(new, "slab", onward)
+    work = [pltpu.VMEM((2, 4 * CH, 256), BF16), pltpu.VMEM((2, CH * 8, 128), F32)]
+    hid, later = call(
         second_kernel, "second", 3 << 30, [SMEM] + [VMEM] * 10,
-        (shape(2, 10, CH, 128), shape(CH, 4, 8, 128)), (VMEM, ANY),
-        [pltpu.VMEM((2, 12, CH, 128), BF16), pltpu.VMEM((2, 8, 64, 192), BF16)] + results,
+        (shape(2, 10, CH, 128), shape(CH, 2, 8, 128)), (VMEM, VMEM),
+        [pltpu.VMEM((2, 12, CH, 128), BF16), pltpu.VMEM((2, 8, 64, 192), BF16)] + work,
     )(flags, old, wup, weave, w1, w2, cols, act, inner_raw, edge_raw, new)
     return call(
-        third_kernel, "third", 1 << 30, [VMEM] * 7 + [ANY],
-        shape(CH, 4, 8, 128), ANY, results, input_output_aliases={7: 0},
-    )(w2, weave, cols, inner_raw, edge_raw, past, hid, out)
+        third_kernel, "third", 1 << 30, [VMEM] * 8, shape(CH, 4, 8, 128), ANY,
+        work + [pltpu.VMEM((CH, 2, 8, 128), BF16), pltpu.SemaphoreType.DMA((3,))],
+    )(w2, weave, cols, inner_raw, edge_raw, past, hid, later)
 
 
 def solution(mesh):

time: 33.6 us -> 33.1 us (0.985)
  Pallas kernels: 14.3 us -> 13.9 us
    ppermute x1, waiting for transfers between devices: 4.94 us -> 4.21 us  [shards(): below = lax.ppermute(low, 'tile', [(i + 1, i) for i in range(tiles - 1)])]
    pallas_call x1, Pallas kernels: 2.32 us -> 3.05 us  [shards(): call(prep_kernel, 'prep', 2 << 30, [VMEM, VMEM, HBM, HBM] + [VMEM] * 5, (...]
    pallas_call x1, Pallas kernels: 5.82 us -> 5.15 us  [shards(): call(second_kernel, 'second', 3 << 30, [SMEM] + [VMEM] * 10, (shape(2, 10...]
    ppermute x1, waiting for transfers between devices: 0.36 us -> 0.95 us  [shards(): past = lax.ppermute(new, 'slab', onward)]
    pallas_call x2, Pallas kernels: 6.13 us -> 5.66 us  [the longest x1 3.12 us: shards(): call(first_kernel, 'first', 3 << 30, [SMEM] + [VMEM] * 8, (shape(4, 12, C...]
  transfers between devices with their start and end apart: 4 -> 4, of which waited for: 2 -> 3; matrix products, arithmetic and copies ran while one was open for 1% -> 1% of each run, Pallas kernels for 35% -> 34%
where the time goes in v1:
time: 33.1 us; the launch traced here: 32.9 us
  Pallas kernels  13.9 us (42%)
  starting transfers between devices  11.8 us (36%)
  waiting for transfers between devices  5.27 us (16%)
  local copies, waits for them, and re-layouts  1.2 us (4%)
  other arithmetic  0.46 us (1%)
    pallas_call x1, Pallas kernels, shards(): call(second_kernel, 'second', 3 << 30, [SMEM] + [VMEM] * 10, (shape(2, 10...  5.15 us
    ppermute x1, waiting for transfers between devices, shards(): below = lax.ppermute(low, 'tile', [(i + 1, i) for i in range(tiles - 1)])  4.21 us
    ppermute x1, starting transfers between devices, shards(): past = lax.ppermute(new, 'slab', onward)  3.92 us
    ppermute x1, starting transfers between devices, shards(): above = lax.ppermute(high, 'tile', [(i, i + 1) for i in range(tiles - 1)])  3.19 us
    pallas_call x1, Pallas kernels, shards(): call(first_kernel, 'first', 3 << 30, [SMEM] + [VMEM] * 8, (shape(4, 12, C...  3.12 us
    pallas_call x1, Pallas kernels, shards(): call(prep_kernel, 'prep', 2 << 30, [VMEM, VMEM, HBM, HBM] + [VMEM] * 5, (...  3.05 us
    ppermute x1, starting transfers between devices, shards(): below = lax.ppermute(low, 'tile', [(i + 1, i) for i in range(tiles - 1)])  2.78 us
    pallas_call x1, Pallas kernels, shards(): call(third_kernel, 'third', 1 << 30, [VMEM] * 8, shape(CH, 4, 8, 128), AN...  2.54 us
  transfers between devices with their start and end apart: 4, of which 3 were waited for; matrix products, arithmetic and copies ran while one was open for 1% of the time, Pallas kernels for 34%

profile of v1, /device:TPU:56, one launch (start us, length us, event | category | flops | bytes accessed | tf_op | source)
XLA Modules:
  0.0 32.9 jit_solution(5236961056086458659)
XLA Ops:
  0.0 1.1 %copy.19 = bf16[192,4,4,64]{0,3,1,2:T(8,128)(2,1)S(1)} copy(bf16[192,4,4,64]{0,3,2,1:T(8,128)(2,1)} %param.10) | data formatting | bytes 786432 | tf_op args[0]
  1.1 0.0 copy-start
  1.1 0.0 copy-start.1
  1.1 0.0 copy-start.2
  1.1 0.0 copy-start.3
  1.1 0.0 copy-start.4
  1.1 0.0 copy-start.5
  1.2 0.0 copy-start.6
  1.2 0.0 copy-start.7
  1.2 0.0 copy-start.8
  1.2 0.1 pad_maximum_fusion.1
  1.4 3.2 %collective-permute-start = (bf16[4,64,384]{2,1,0:T(8,128)(2,1)S(1)}, bf16[4,64,384]{2,1,0:T(8,128)(2,1)S(1)}, u32[]{:S(2)}, u32[]{:S(2)}) collective-permute-start(bf16[4,64,384]{2,1,0:T(8,128)(2,1)S(1)} %pad_maximum_fusion.1), channel_id=1, source_target_pairs={{0,1},{1,2},{2,3},{3,4},{4,5},{5,6},{6,7},{7,8},{8,9},{9,10},{10,1... | collective-permute-start | bytes 589832 | tf_op jit(solution)/shard_map/ppermute | solution.py:253
  4.5 0.1 pad_maximum_fusion.2
  4.7 2.8 %collective-permute-start.1 = (bf16[4,64,384]{2,1,0:T(8,128)(2,1)S(1)}, bf16[4,64,384]{2,1,0:T(8,128)(2,1)S(1)}, u32[]{:S(2)}, u32[]{:S(2)}) collective-permute-start(bf16[4,64,384]{2,1,0:T(8,128)(2,1)S(1)} %pad_maximum_fusion.2), channel_id=1, source_target_pairs={{1,0},{2,1},{3,2},{4,3},{5,4},{6,5},{7,6},{8,7},{9,8},{10,9},{11,1... | collective-permute-start | bytes 589832 | tf_op jit(solution)/shard_map/ppermute | solution.py:254
  7.5 0.1 fusion.1
  7.6 0.1 pad_add_fusion.flags
  7.6 0.0 copy-done
  7.7 0.0 copy-done.1
  7.7 0.0 copy-done.2
  7.7 0.0 copy-done.3
  7.7 3.1 %prep.1 = (bf16[4,384,192]{2,1,0:T(8,128)(2,1)S(1)}, bf16[288,864]{1,0:T(8,128)(2,1)S(1)}, bf16[288,864]{1,0:T(8,128)(2,1)S(1)}, f32[5,96,128]{2,1,0:T(8,128)S(1...) custom-call(bf16[4,4,64,192]{3,2,1,0:T(8,128)(2,1)S(1)} %bitcast.34,, ...), custom_call_target="tpu_custom_call" | custom-call | flops 2147483648 | bytes 4194304 | tf_op jit(solution)/shard_map/prep/pallas_call | solution.py:255
  10.8 0.0 collective-permute-done.above_ref
  10.8 4.2 %collective-permute-done.1.below_ref = bf16[4,64,384]{2,1,0:T(8,128)(2,1)S(1)} collective-permute-done((bf16[4,64,384]{2,1,0:T(8,128)(2,1)S(1)}, bf16[4,64,384]{2,1,0:T(8,128)(2,1)S(1)}, u32[]{:S(2)}, u32[]{:S(2)}) %collective-permute-start.1) | collective-permute-done | bytes 196640 | tf_op jit(solution)/shard_map/ppermute | solution.py:254
  15.0 0.1 pad_maximum_fusion
  15.1 1.9 %collective-permute-start.3 = (bf16[2,4,64,384]{3,2,1,0:T(8,128)(2,1)S(1)}, bf16[2,4,64,384]{3,2,1,0:T(8,128)(2,1)S(1)}, u32[]{:S(2)}, u32[]{:S(2)}) collective-permute-start(bf16[2,4,64,384]{3,2,1,0:T(8,128)(2,1)S(1)} %pad_maximum_fusion), channel_id=1, source_target_pairs={{0,16},{16,32},{32,48},{48,64},{64,80},{80,96},{96,112},{1,17},{17... | collective-permute-start | bytes 1179656 | tf_op jit(solution)/shard_map/ppermute | solution.py:264
  17.0 0.0 copy-start.9
  17.1 3.1 %first.1 = (bf16[4,12,96,128]{3,2,1,0:T(8,128)(2,1)S(1)}, bf16[4,2,96,128]{3,2,1,0:T(8,128)(2,1)S(1)}, bf16[2,10,96,128]{3,2,1,0:T(8,128)(2,1)S(1)}) custom-call(s32[3]{0:T(128)S(1)} %pad_add_fusion.flags, bf16[4,4,64,192]{3,2,1,0:T(8,128)(2,1)S(1)} %bitcast.35, bf16[4,64,384]{2,1,0:T(8,128)(2,1)S(1)} %collective-permute-done.above_ref, ...), custom_call_target="tpu_custom_call" | custom-call | flops 3221225472 | bytes 4194304 | tf_op jit(solution)/shard_map/first/pallas_call | solution.py:265
  20.2 3.9 %collective-permute-start.2 = (bf16[2,10,96,128]{3,2,1,0:T(8,128)(2,1)S(1)}, bf16[2,10,96,128]{3,2,1,0:T(8,128)(2,1)S(1)}, u32[]{:S(2)}, u32[]{:S(2)}) collective-permute-start(bf16[2,10,96,128]{3,2,1,0:T(8,128)(2,1)S(1)} %get-tuple-element.25.new_ref), channel_id=1, source_target_pairs={{0,16},{16,32},{32,48},{48,64},{64,80},{80,96},{96,112},{1,17},{17... | collective-permute-start | bytes 1474568 | tf_op jit(solution)/shard_map/ppermute | solution.py:269
  24.1 0.1 collective-permute-done.3.old_ref
  24.2 5.2 %second.1 = (bf16[2,10,96,128]{3,2,1,0:T(8,128)(2,1)S(1)}, bf16[96,2,8,128]{3,2,1,0:T(8,128)(2,1)S(1)}) custom-call(s32[3]{0:T(128)S(1)} %pad_add_fusion.flags, bf16[2,4,64,384]{3,2,1,0:T(8,128)(2,1)S(1)} %collective-permute-done.3.old_ref, bf16[4,384,192]{2,1,0:T(8,128)(2,1)S(1)} %get-tuple-element.20.wup_ref, bf16[256,256]{1,0:T(8,128)(2,1)S(1)} %copy-done.9, ...), custom_call_target="tpu_custom_call" | custom-call | flops 3221225472 | bytes 4194304 | tf_op jit(solution)/shard_map/second/pallas_call | solution.py:271
  29.4 1.0 %collective-permute-done.2.past_ref = bf16[2,10,96,128]{3,2,1,0:T(8,128)(2,1)S(1)} collective-permute-done((bf16[2,10,96,128]{3,2,1,0:T(8,128)(2,1)S(1)}, bf16[2,10,96,128]{3,2,1,0:T(8,128)(2,1)S(1)}, u32[]{:S(2)}, u32[]{:S(2)}) %collective-permute-start.2) | collective-permute-done | bytes 491552 | tf_op jit(solution)/shard_map/ppermute | solution.py:269
  30.3 2.5 %third.1 = bf16[96,4,8,128]{3,2,1,0:T(8,128)(2,1)} custom-call(bf16[288,864]{1,0:T(8,128)(2,1)S(1)} %get-tuple-element.17.w2_ref, bf16[256,256]{1,0:T(8,128)(2,1)S(1)} %copy-done.9, f32[5,96,128]{2,1,0:T(8,128)S(1)} %get-tuple-element.18.cols_ref, bf16[4,6,96,128]{3,2,1,0:T(8,128)(2,1)S(1)} %get-tuple-element.19.inner_ref, ...), custom_call_target="tpu_custom_call" | custom-call | flops 1073741824 | bytes 4194304 | tf_op jit(solution)/shard_map/third/pallas_call | solution.py:276
  (9 shorter events, 0.1 us)
Async XLA Ops:
  1.1 6.6 %copy-start = (bf16[192,4,4,64]{0,3,2,1:T(8,128)(2,1)S(1)}, bf16[192,4,4,64]{0,3,2,1:T(8,128)(2,1)}, u32[]{:S(2)}) copy-start(bf16[192,4,4,64]{0,3,2,1:T(8,128)(2,1)} %param.10) | copy-start | bytes 1179652
  1.1 6.6 %copy-start.1 = (bf16[3,3,96,288]{3,2,1,0:T(8,128)(2,1)S(1)}, bf16[3,3,96,288]{3,2,1,0:T(8,128)(2,1)}, u32[]{:S(2)}) copy-start(bf16[3,3,96,288]{3,2,1,0:T(8,128)(2,1)} %one_ref.1) | copy-start | bytes 1492996
  1.1 6.6 %copy-start.2 = (bf16[3,3,96,288]{3,2,1,0:T(8,128)(2,1)S(1)}, bf16[3,3,96,288]{3,2,1,0:T(8,128)(2,1)}, u32[]{:S(2)}) copy-start(bf16[3,3,96,288]{3,2,1,0:T(8,128)(2,1)} %two_ref.1) | copy-start | bytes 1492996
  1.1 6.5 %copy-start.3 = (bf16[3,3,96,192]{3,2,1,0:T(8,128)(2,1)S(1)}, bf16[3,3,96,192]{3,2,1,0:T(8,128)(2,1)}, u32[]{:S(2)}) copy-start(bf16[3,3,96,192]{3,2,1,0:T(8,128)(2,1)} %up_ref.1) | copy-start | bytes 995332
  1.1 6.5 %copy-start.4 = (f32[96]{0:T(128)S(1)}, f32[96]{0:T(128)}, u32[]{:S(2)}) copy-start(f32[96]{0:T(128)} %param.12) | copy-start | bytes 1156
  1.1 6.5 %copy-start.5 = (f32[96]{0:T(128)S(1)}, f32[96]{0:T(128)}, u32[]{:S(2)}) copy-start(f32[96]{0:T(128)} %param.13) | copy-start | bytes 1156
  1.2 6.5 %copy-start.6 = (f32[96]{0:T(128)S(1)}, f32[96]{0:T(128)}, u32[]{:S(2)}) copy-start(f32[96]{0:T(128)} %param.15) | copy-start | bytes 1156
  1.2 6.5 %copy-start.7 = (f32[96]{0:T(128)S(1)}, f32[96]{0:T(128)}, u32[]{:S(2)}) copy-start(f32[96]{0:T(128)} %param.16) | copy-start | bytes 1156
  1.2 6.5 %copy-start.8 = (f32[96]{0:T(128)S(1)}, f32[96]{0:T(128)}, u32[]{:S(2)}) copy-start(f32[96]{0:T(128)} %param.18) | copy-start | bytes 1156
  1.4 9.4 %collective-permute-start = (bf16[4,64,384]{2,1,0:T(8,128)(2,1)S(1)}, bf16[4,64,384]{2,1,0:T(8,128)(2,1)S(1)}, u32[]{:S(2)}, u32[]{:S(2)}) collective-permute-start(bf16[4,64,384]{2,1,0:T(8,128)(2,1)S(1)} %pad_maximum_fusion.1), channel_id=1, source_target_pairs={{0,1},{1,2},{2,3},{3,4},{4,5},{5,6},{6,7},{7,8},{8,9},{9,10},{10,1... | collective-permute-start | bytes 589832 | tf_op jit(solution)/shard_map/ppermute | solution.py:253
  4.7 10.4 %collective-permute-start.1 = (bf16[4,64,384]{2,1,0:T(8,128)(2,1)S(1)}, bf16[4,64,384]{2,1,0:T(8,128)(2,1)S(1)}, u32[]{:S(2)}, u32[]{:S(2)}) collective-permute-start(bf16[4,64,384]{2,1,0:T(8,128)(2,1)S(1)} %pad_maximum_fusion.2), channel_id=1, source_target_pairs={{1,0},{2,1},{3,2},{4,3},{5,4},{6,5},{7,6},{8,7},{9,8},{10,9},{11,1... | collective-permute-start | bytes 589832 | tf_op jit(solution)/shard_map/ppermute | solution.py:254
  15.1 9.1 %collective-permute-start.3 = (bf16[2,4,64,384]{3,2,1,0:T(8,128)(2,1)S(1)}, bf16[2,4,64,384]{3,2,1,0:T(8,128)(2,1)S(1)}, u32[]{:S(2)}, u32[]{:S(2)}) collective-permute-start(bf16[2,4,64,384]{3,2,1,0:T(8,128)(2,1)S(1)} %pad_maximum_fusion), channel_id=1, source_target_pairs={{0,16},{16,32},{32,48},{48,64},{64,80},{80,96},{96,112},{1,17},{17... | collective-permute-start | bytes 1179656 | tf_op jit(solution)/shard_map/ppermute | solution.py:264
  17.0 7.2 %copy-start.9 = (bf16[256,256]{1,0:T(8,128)(2,1)S(1)}, bf16[256,256]{1,0:T(8,128)(2,1)}, u32[]{:S(2)}) copy-start(bf16[256,256]{1,0:T(8,128)(2,1)} %constant.13.clone.weave_ref) | copy-start | bytes 393220
  20.2 10.1 %collective-permute-start.2 = (bf16[2,10,96,128]{3,2,1,0:T(8,128)(2,1)S(1)}, bf16[2,10,96,128]{3,2,1,0:T(8,128)(2,1)S(1)}, u32[]{:S(2)}, u32[]{:S(2)}) collective-permute-start(bf16[2,10,96,128]{3,2,1,0:T(8,128)(2,1)S(1)} %get-tuple-element.25.new_ref), channel_id=1, source_target_pairs={{0,16},{16,32},{32,48},{48,64},{64,80},{80,96},{96,112},{1,17},{17... | collective-permute-start | bytes 1474568 | tf_op jit(solution)/shard_map/ppermute | solution.py:269

commit v2 on v1

--- a/solution.py
+++ b/solution.py
@@ -10,7 +10,6 @@
 BF16 = jnp.bfloat16
 CH = 96
 VMEM = pl.BlockSpec(memory_space=pltpu.VMEM)
-SMEM = pl.BlockSpec(memory_space=pltpu.SMEM)
 ANY = pl.BlockSpec(memory_space=pl.ANY)
 HBM = pl.BlockSpec(memory_space=pltpu.HBM)
 
@@ -38,17 +37,21 @@
 
 
 def up_tile(top, bottom, p, wup_ref, cols_ref, emit):
-    lane = lanes_of((CH, 128))
+    lane = lanes_of((16, 128))
     dims = (((1,), (1,)), ((), ()))
     u = lax.dot_general(wup_ref[2 * p], top.reshape(256, 192), dims, preferred_element_type=F32)
     u = u + lax.dot_general(wup_ref[2 * p + 1], bottom.reshape(256, 192), dims, preferred_element_type=F32)
     for g in range(2):
-        part = u[:, 128 * g:128 * g + 128]
-        even = part[:CH] + jnp.where(lane % 64 == 0, 0.0, pltpu.roll(part[CH:2 * CH], 1, 1)) + cols_ref[0]
-        odd = part[2 * CH:3 * CH] + jnp.where(lane % 64 == 63, 0.0, pltpu.roll(part[3 * CH:], 127, 1)) + cols_ref[0]
-        even, odd = even.astype(BF16).astype(F32), odd.astype(BF16).astype(F32)
-        emit(2 * g, jnp.where(lane < 64, even, pltpu.roll(odd, 64, 1)))
-        emit(2 * g + 1, jnp.where(lane < 64, pltpu.roll(even, 64, 1), odd))
+        first, second = [], []
+        for k in range(0, CH, 16):
+            a, b, c, d = (u[4 * k + m:4 * k + m + 16, 128 * g:128 * g + 128] for m in (0, 16, 32, 48))
+            even = a + jnp.where(lane % 64 == 0, 0.0, pltpu.roll(b, 1, 1)) + cols_ref[0, k:k + 16]
+            odd = c + jnp.where(lane % 64 == 63, 0.0, pltpu.roll(d, 127, 1)) + cols_ref[0, k:k + 16]
+            even, odd = even.astype(BF16).astype(F32), odd.astype(BF16).astype(F32)
+            first.append(jnp.where(lane < 64, even, pltpu.roll(odd, 64, 1)))
+            second.append(jnp.where(lane < 64, pltpu.roll(even, 64, 1), odd))
+        emit(2 * g, jnp.concatenate(first, axis=0))
+        emit(2 * g + 1, jnp.concatenate(second, axis=0))
 
 
 def conv_pair(src, w_ref, f, r, s):
@@ -57,16 +60,18 @@
         for t in range(3) for a in range(3)
     ]
     sums = jnp.dot(w_ref[...], jnp.concatenate(taps, axis=0), preferred_element_type=F32)
-    lane = lanes_of((CH, 128))
+    lane = lanes_of((16, 128))
     edge = jnp.logical_or(lane == 0, lane == 127)
     rows = []
     for h in range(2):
-        part = sums[:, 128 * h:128 * h + 128]
-        left, right = part[:CH], part[2 * CH:]
-        near = pltpu.roll(jnp.where(lane < 64, left, right), 64, 1)
-        far = jnp.where(lane < 64, right, left)
-        far = jnp.where(lane < 64, pltpu.roll(far, 65, 1), pltpu.roll(far, 63, 1))
-        rows.append(part[CH:2 * CH] + near + jnp.where(edge, 0.0, far))
+        blocks = []
+        for k in range(0, 3 * CH, 48):
+            left, middle, right = (sums[k + b:k + b + 16, 128 * h:128 * h + 128] for b in (0, 16, 32))
+            near = pltpu.roll(jnp.where(lane < 64, left, right), 64, 1)
+            far = jnp.where(lane < 64, right, left)
+            far = jnp.where(lane < 64, pltpu.roll(far, 65, 1), pltpu.roll(far, 63, 1))
+            blocks.append(middle + near + jnp.where(edge, 0.0, far))
+        rows.append(jnp.concatenate(blocks, axis=0))
     return rows
 
 
@@ -120,7 +125,8 @@
                 tap = up_ref[1, b].astype(F32) + up_ref[2 if n == 1 else 0, b].astype(F32)
             taps.append(tap)
         for m, tap in enumerate((taps[1] + taps[2], taps[0], taps[0] + taps[1], taps[2])):
-            wup_ref[n, CH * m:CH * m + CH, :] = tap.astype(BF16)
+            for k in range(0, CH, 16):
+                wup_ref[n, 4 * k + 16 * m:4 * k + 16 * m + 16, :] = tap[k:k + 16].astype(BF16)
     for n, ref in enumerate((upb_ref, g1_ref, b1_ref, g2_ref, b2_ref)):
         cols_ref[n] = jnp.broadcast_to(ref[...], (128, CH)).T
     for k in range(3):
@@ -134,14 +140,21 @@
         load.wait()
         for b in range(3):
             pieces = [src_ref[t, a][:, CH * b:CH * b + CH] for t in range(3) for a in range(3)]
-            dst_ref[CH * b:CH * b + CH, :] = jnp.concatenate(pieces, axis=1)
+            rows = jnp.concatenate(pieces, axis=1)
+            for k in range(0, CH, 16):
+                dst_ref[3 * k + 16 * b:3 * k + 16 * b + 16, :] = rows[k:k + 16]
     for f in range(2):
         hidden_frame(lambda i, r: act_ref[i, r], f, ((0, 1), (2, 3)), w1_ref, cols_ref, hid_ref, None, None)
 
 
-def first_kernel(flags, x_ref, above_ref, below_ref, wup_ref, w1_ref, cols_ref, inner_ref, inner_hid_ref,
+def surroundings():
+    place = lax.axis_index("tile")
+    return place > 0, place < lax.axis_size("tile") - 1, lax.axis_index("slab") > 0
+
+
+def first_kernel(x_ref, above_ref, below_ref, wup_ref, w1_ref, cols_ref, inner_ref, inner_hid_ref,
                  act_ref, edge_ref, hid_ref):
-    has_top, has_bottom = flags[0] > 0, flags[1] > 0
+    has_top, has_bottom, _ = surroundings()
     act_ref[:, 3:9] = inner_ref[...]
     hid_ref[:, 3:7] = inner_hid_ref[...]
     above, below = above_ref[...], below_ref[...]
@@ -178,9 +191,9 @@
     return load
 
 
-def second_kernel(flags, old_ref, wup_ref, weave_ref, w1_ref, w2_ref, cols_ref, act_ref, inner_ref, edge_ref, new_ref,
+def second_kernel(old_ref, wup_ref, weave_ref, w1_ref, w2_ref, cols_ref, act_ref, inner_ref, edge_ref, new_ref,
                   hid_ref, res_ref, past_act_ref, rows_ref, both_ref, mix_ref):
-    has_top, has_bottom, has_old = flags[0] > 0, flags[1] > 0, flags[2] > 0
+    has_top, has_bottom, has_old = surroundings()
     for k in range(4):
         both = old_ref[:, k]
         rows_ref[:, 2 * k] = both[..., :192]
@@ -259,20 +272,18 @@
         [pltpu.VMEM((3, 3, CH, 3 * CH), BF16), pltpu.VMEM((3, 3, CH, 3 * CH), BF16), pltpu.SemaphoreType.DMA((2,))],
     )(x, up_weight, conv_one, conv_two, *(v.reshape(1, CH) for v in (up_bias, gain_one, bias_one, gain_two, bias_two)))
     weave = jnp.asarray(weave_matrix(), BF16)
-    place, age = lax.axis_index("tile"), lax.axis_index("slab")
-    flags = jnp.stack([place, tiles - 1 - place, age]).astype(jnp.int32)
     old = lax.ppermute(jnp.stack([above[2:], low[2:], high[2:], below[2:]], axis=1), "slab", onward)
     act, edge_raw, new = call(
-        first_kernel, "first", 3 << 30, [SMEM] + [VMEM] * 8,
+        first_kernel, "first", 3 << 30, [VMEM] * 8,
         (shape(4, 12, CH, 128), shape(4, 2, CH, 128), shape(2, 10, CH, 128)), (VMEM,) * 3,
-    )(flags, x, above, below, wup, w1, cols, inner_act, inner_hid)
+    )(x, above, below, wup, w1, cols, inner_act, inner_hid)
     past = lax.ppermute(new, "slab", onward)
     work = [pltpu.VMEM((2, 4 * CH, 256), BF16), pltpu.VMEM((2, CH * 8, 128), F32)]
     hid, later = call(
-        second_kernel, "second", 3 << 30, [SMEM] + [VMEM] * 10,
+        second_kernel, "second", 3 << 30, [VMEM] * 10,
         (shape(2, 10, CH, 128), shape(CH, 2, 8, 128)), (VMEM, VMEM),
         [pltpu.VMEM((2, 12, CH, 128), BF16), pltpu.VMEM((2, 8, 64, 192), BF16)] + work,
-    )(flags, old, wup, weave, w1, w2, cols, act, inner_raw, edge_raw, new)
+    )(old, wup, weave, w1, w2, cols, act, inner_raw, edge_raw, new)
     return call(
         third_kernel, "third", 1 << 30, [VMEM] * 8, shape(CH, 4, 8, 128), ANY,
         work + [pltpu.VMEM((CH, 2, 8, 128), BF16), pltpu.SemaphoreType.DMA((3,))],

time: 33.1 us -> 32.5 us (0.982)
  Pallas kernels: 13.9 us -> 12.7 us
  waiting for transfers between devices: 5.27 us -> 5.88 us
    pallas_call x2, Pallas kernels: 8.27 us -> 7.13 us  [the longest x1 4.53 us: shards(): call(second_kernel, 'second', 3 << 30, [VMEM] * 10, (shape(2, 10, CH, 128...]
    ppermute x1, waiting for transfers between devices: 0.1 us -> 0.61 us  [shards(): lax.ppermute(jnp.stack([above[2:], low[2:], high[2:], below[2:]], axis=1)...]
  transfers between devices with their start and end apart: 4 -> 4, of which waited for: 3 -> 3; matrix products, arithmetic and copies ran while one was open for 1% -> 1% of each run, Pallas kernels for 34% -> 32%
where the time goes in v2:
time: 32.5 us; the launch traced here: 32.3 us
  Pallas kernels  12.7 us (39%)
  starting transfers between devices  11.8 us (36%)
  waiting for transfers between devices  5.88 us (18%)
  local copies, waits for them, and re-layouts  1.2 us (4%)
  other arithmetic  0.39 us (1%)
    pallas_call x1, Pallas kernels, shards(): call(second_kernel, 'second', 3 << 30, [VMEM] * 10, (shape(2, 10, CH, 128...  4.53 us
    ppermute x1, waiting for transfers between devices, shards(): below = lax.ppermute(low, 'tile', [(i + 1, i) for i in range(tiles - 1)])  4.21 us
    ppermute x1, starting transfers between devices, shards(): past = lax.ppermute(new, 'slab', onward)  3.93 us
    ppermute x1, starting transfers between devices, shards(): above = lax.ppermute(high, 'tile', [(i, i + 1) for i in range(tiles - 1)])  3.19 us
    pallas_call x1, Pallas kernels, shards(): call(prep_kernel, 'prep', 2 << 30, [VMEM, VMEM, HBM, HBM] + [VMEM] * 5, (...  3.12 us
    ppermute x1, starting transfers between devices, shards(): below = lax.ppermute(low, 'tile', [(i + 1, i) for i in range(tiles - 1)])  2.78 us
    pallas_call x1, Pallas kernels, shards(): call(first_kernel, 'first', 3 << 30, [VMEM] * 8, (shape(4, 12, CH, 128),...  2.6 us
    pallas_call x1, Pallas kernels, shards(): call(third_kernel, 'third', 1 << 30, [VMEM] * 8, shape(CH, 4, 8, 128), AN...  2.44 us
  transfers between devices with their start and end apart: 4, of which 3 were waited for; matrix products, arithmetic and copies ran while one was open for 1% of the time, Pallas kernels for 32%

profile of v2, /device:TPU:56, one launch (start us, length us, event | category | flops | bytes accessed | tf_op | source)
XLA Modules:
  0.0 32.3 jit_solution(129084433780792020)
XLA Ops:
  0.0 1.1 %copy.19 = bf16[192,4,4,64]{0,3,1,2:T(8,128)(2,1)S(1)} copy(bf16[192,4,4,64]{0,3,2,1:T(8,128)(2,1)} %param.10) | data formatting | bytes 786432 | tf_op args[0]
  1.1 0.0 copy-start
  1.1 0.0 copy-start.1
  1.1 0.0 copy-start.2
  1.1 0.0 copy-start.3
  1.1 0.0 copy-start.4
  1.1 0.0 copy-start.5
  1.2 0.0 copy-start.6
  1.2 0.0 copy-start.7
  1.2 0.0 copy-start.8
  1.2 0.1 pad_maximum_fusion.1
  1.3 3.2 %collective-permute-start = (bf16[4,64,384]{2,1,0:T(8,128)(2,1)S(1)}, bf16[4,64,384]{2,1,0:T(8,128)(2,1)S(1)}, u32[]{:S(2)}, u32[]{:S(2)}) collective-permute-start(bf16[4,64,384]{2,1,0:T(8,128)(2,1)S(1)} %pad_maximum_fusion.1), channel_id=1, source_target_pairs={{0,1},{1,2},{2,3},{3,4},{4,5},{5,6},{6,7},{7,8},{8,9},{9,10},{10,1... | collective-permute-start | bytes 589832 | tf_op jit(solution)/shard_map/ppermute | solution.py:266
  4.5 0.1 pad_maximum_fusion.2
  4.7 2.8 %collective-permute-start.1 = (bf16[4,64,384]{2,1,0:T(8,128)(2,1)S(1)}, bf16[4,64,384]{2,1,0:T(8,128)(2,1)S(1)}, u32[]{:S(2)}, u32[]{:S(2)}) collective-permute-start(bf16[4,64,384]{2,1,0:T(8,128)(2,1)S(1)} %pad_maximum_fusion.2), channel_id=1, source_target_pairs={{1,0},{2,1},{3,2},{4,3},{5,4},{6,5},{7,6},{8,7},{9,8},{10,9},{11,1... | collective-permute-start | bytes 589832 | tf_op jit(solution)/shard_map/ppermute | solution.py:267
  7.5 0.1 fusion.1
  7.6 0.0 copy-done
  7.6 0.0 copy-done.1
  7.6 0.0 copy-done.2
  7.6 0.0 copy-done.3
  7.6 0.0 copy-done.4
  7.7 3.1 %prep.1 = (bf16[4,384,192]{2,1,0:T(8,128)(2,1)S(1)}, bf16[288,864]{1,0:T(8,128)(2,1)S(1)}, bf16[288,864]{1,0:T(8,128)(2,1)S(1)}, f32[5,96,128]{2,1,0:T(8,128)S(1...) custom-call(bf16[4,4,64,192]{3,2,1,0:T(8,128)(2,1)S(1)} %bitcast.31,, ...), custom_call_target="tpu_custom_call" | custom-call | flops 2147483648 | bytes 4194304 | tf_op jit(solution)/shard_map/prep/pallas_call | solution.py:268
  10.8 0.0 collective-permute-done.above_ref
  10.8 4.2 %collective-permute-done.1.below_ref = bf16[4,64,384]{2,1,0:T(8,128)(2,1)S(1)} collective-permute-done((bf16[4,64,384]{2,1,0:T(8,128)(2,1)S(1)}, bf16[4,64,384]{2,1,0:T(8,128)(2,1)S(1)}, u32[]{:S(2)}, u32[]{:S(2)}) %collective-permute-start.1) | collective-permute-done | bytes 196640 | tf_op jit(solution)/shard_map/ppermute | solution.py:267
  15.0 0.1 pad_maximum_fusion
  15.1 1.9 %collective-permute-start.3 = (bf16[2,4,64,384]{3,2,1,0:T(8,128)(2,1)S(1)}, bf16[2,4,64,384]{3,2,1,0:T(8,128)(2,1)S(1)}, u32[]{:S(2)}, u32[]{:S(2)}) collective-permute-start(bf16[2,4,64,384]{3,2,1,0:T(8,128)(2,1)S(1)} %pad_maximum_fusion), channel_id=1, source_target_pairs={{0,16},{16,32},{32,48},{48,64},{64,80},{80,96},{96,112},{1,17},{17... | collective-permute-start | bytes 1179656 | tf_op jit(solution)/shard_map/ppermute | solution.py:275
  17.0 0.0 copy-start.9
  17.0 2.6 %first.1 = (bf16[4,12,96,128]{3,2,1,0:T(8,128)(2,1)S(1)}, bf16[4,2,96,128]{3,2,1,0:T(8,128)(2,1)S(1)}, bf16[2,10,96,128]{3,2,1,0:T(8,128)(2,1)S(1)}) custom-call(bf16[4,4,64,192]{3,2,1,0:T(8,128)(2,1)S(1)} %bitcast.32, bf16[4,64,384]{2,1,0:T(8,128)(2,1)S(1)} %collective-permute-done.above_ref, bf16[4,64,384]{2,1,0:T(8,128)(2,1)S(1)} %collective-permute-done.1.below_ref, ...), custom_call_target="tpu_custom_call" | custom-call | flops 3221225472 | bytes 4194304 | tf_op jit(solution)/shard_map/first/pallas_call | solution.py:276
  19.7 3.9 %collective-permute-start.2 = (bf16[2,10,96,128]{3,2,1,0:T(8,128)(2,1)S(1)}, bf16[2,10,96,128]{3,2,1,0:T(8,128)(2,1)S(1)}, u32[]{:S(2)}, u32[]{:S(2)}) collective-permute-start(bf16[2,10,96,128]{3,2,1,0:T(8,128)(2,1)S(1)} %get-tuple-element.25.new_ref), channel_id=1, source_target_pairs={{0,16},{16,32},{32,48},{48,64},{64,80},{80,96},{96,112},{1,17},{17... | collective-permute-start | bytes 1474568 | tf_op jit(solution)/shard_map/ppermute | solution.py:280
  23.6 0.6 %collective-permute-done.3.old_ref = bf16[2,4,64,384]{3,2,1,0:T(8,128)(2,1)S(1)} collective-permute-done((bf16[2,4,64,384]{3,2,1,0:T(8,128)(2,1)S(1)}, bf16[2,4,64,384]{3,2,1,0:T(8,128)(2,1)S(1)}, u32[]{:S(2)}, u32[]{:S(2)}) %collective-permute-start.3) | collective-permute-done | bytes 393248 | tf_op jit(solution)/shard_map/ppermute | solution.py:275
  24.2 4.5 %second.1 = (bf16[2,10,96,128]{3,2,1,0:T(8,128)(2,1)S(1)}, bf16[96,2,8,128]{3,2,1,0:T(8,128)(2,1)S(1)}) custom-call(bf16[2,4,64,384]{3,2,1,0:T(8,128)(2,1)S(1)} %collective-permute-done.3.old_ref, bf16[4,384,192]{2,1,0:T(8,128)(2,1)S(1)} %get-tuple-element.20.wup_ref, bf16[256,256]{1,0:T(8,128)(2,1)S(1)} %copy-done.9, ...), custom_call_target="tpu_custom_call" | custom-call | flops 3221225472 | bytes 4194304 | tf_op jit(solution)/shard_map/second/pallas_call | solution.py:282
  28.7 1.1 %collective-permute-done.2.past_ref = bf16[2,10,96,128]{3,2,1,0:T(8,128)(2,1)S(1)} collective-permute-done((bf16[2,10,96,128]{3,2,1,0:T(8,128)(2,1)S(1)}, bf16[2,10,96,128]{3,2,1,0:T(8,128)(2,1)S(1)}, u32[]{:S(2)}, u32[]{:S(2)}) %collective-permute-start.2) | collective-permute-done | bytes 491552 | tf_op jit(solution)/shard_map/ppermute | solution.py:280
  29.8 2.4 %third.1 = bf16[96,4,8,128]{3,2,1,0:T(8,128)(2,1)} custom-call(bf16[288,864]{1,0:T(8,128)(2,1)S(1)} %get-tuple-element.17.w2_ref, bf16[256,256]{1,0:T(8,128)(2,1)S(1)} %copy-done.9, f32[5,96,128]{2,1,0:T(8,128)S(1)} %get-tuple-element.18.cols_ref, bf16[4,6,96,128]{3,2,1,0:T(8,128)(2,1)S(1)} %get-tuple-element.19.inner_ref, ...), custom_call_target="tpu_custom_call" | custom-call | flops 1073741824 | bytes 4194304 | tf_op jit(solution)/shard_map/third/pallas_call | solution.py:287
  (8 shorter events, 0.1 us)
Async XLA Ops:
  1.1 6.5 %copy-start = (bf16[192,4,4,64]{0,3,2,1:T(8,128)(2,1)S(1)}, bf16[192,4,4,64]{0,3,2,1:T(8,128)(2,1)}, u32[]{:S(2)}) copy-start(bf16[192,4,4,64]{0,3,2,1:T(8,128)(2,1)} %param.10) | copy-start | bytes 1179652
  1.1 6.5 %copy-start.1 = (bf16[3,3,96,288]{3,2,1,0:T(8,128)(2,1)S(1)}, bf16[3,3,96,288]{3,2,1,0:T(8,128)(2,1)}, u32[]{:S(2)}) copy-start(bf16[3,3,96,288]{3,2,1,0:T(8,128)(2,1)} %one_ref.1) | copy-start | bytes 1492996
  1.1 6.5 %copy-start.2 = (bf16[3,3,96,288]{3,2,1,0:T(8,128)(2,1)S(1)}, bf16[3,3,96,288]{3,2,1,0:T(8,128)(2,1)}, u32[]{:S(2)}) copy-start(bf16[3,3,96,288]{3,2,1,0:T(8,128)(2,1)} %two_ref.1) | copy-start | bytes 1492996
  1.1 6.5 %copy-start.3 = (bf16[3,3,96,192]{3,2,1,0:T(8,128)(2,1)S(1)}, bf16[3,3,96,192]{3,2,1,0:T(8,128)(2,1)}, u32[]{:S(2)}) copy-start(bf16[3,3,96,192]{3,2,1,0:T(8,128)(2,1)} %up_ref.1) | copy-start | bytes 995332
  1.1 6.5 %copy-start.4 = (f32[96]{0:T(128)S(1)}, f32[96]{0:T(128)}, u32[]{:S(2)}) copy-start(f32[96]{0:T(128)} %param.12) | copy-start | bytes 1156
  1.1 6.5 %copy-start.5 = (f32[96]{0:T(128)S(1)}, f32[96]{0:T(128)}, u32[]{:S(2)}) copy-start(f32[96]{0:T(128)} %param.13) | copy-start | bytes 1156
  1.2 6.5 %copy-start.6 = (f32[96]{0:T(128)S(1)}, f32[96]{0:T(128)}, u32[]{:S(2)}) copy-start(f32[96]{0:T(128)} %param.15) | copy-start | bytes 1156
  1.2 6.5 %copy-start.7 = (f32[96]{0:T(128)S(1)}, f32[96]{0:T(128)}, u32[]{:S(2)}) copy-start(f32[96]{0:T(128)} %param.16) | copy-start | bytes 1156
  1.2 6.5 %copy-start.8 = (f32[96]{0:T(128)S(1)}, f32[96]{0:T(128)}, u32[]{:S(2)}) copy-start(f32[96]{0:T(128)} %param.18) | copy-start | bytes 1156
  1.3 9.4 %collective-permute-start = (bf16[4,64,384]{2,1,0:T(8,128)(2,1)S(1)}, bf16[4,64,384]{2,1,0:T(8,128)(2,1)S(1)}, u32[]{:S(2)}, u32[]{:S(2)}) collective-permute-start(bf16[4,64,384]{2,1,0:T(8,128)(2,1)S(1)} %pad_maximum_fusion.1), channel_id=1, source_target_pairs={{0,1},{1,2},{2,3},{3,4},{4,5},{5,6},{6,7},{7,8},{8,9},{9,10},{10,1... | collective-permute-start | bytes 589832 | tf_op jit(solution)/shard_map/ppermute | solution.py:266
  4.7 10.4 %collective-permute-start.1 = (bf16[4,64,384]{2,1,0:T(8,128)(2,1)S(1)}, bf16[4,64,384]{2,1,0:T(8,128)(2,1)S(1)}, u32[]{:S(2)}, u32[]{:S(2)}) collective-permute-start(bf16[4,64,384]{2,1,0:T(8,128)(2,1)S(1)} %pad_maximum_fusion.2), channel_id=1, source_target_pairs={{1,0},{2,1},{3,2},{4,3},{5,4},{6,5},{7,6},{8,7},{9,8},{10,9},{11,1... | collective-permute-start | bytes 589832 | tf_op jit(solution)/shard_map/ppermute | solution.py:267
  15.1 9.1 %collective-permute-start.3 = (bf16[2,4,64,384]{3,2,1,0:T(8,128)(2,1)S(1)}, bf16[2,4,64,384]{3,2,1,0:T(8,128)(2,1)S(1)}, u32[]{:S(2)}, u32[]{:S(2)}) collective-permute-start(bf16[2,4,64,384]{3,2,1,0:T(8,128)(2,1)S(1)} %pad_maximum_fusion), channel_id=1, source_target_pairs={{0,16},{16,32},{32,48},{48,64},{64,80},{80,96},{96,112},{1,17},{17... | collective-permute-start | bytes 1179656 | tf_op jit(solution)/shard_map/ppermute | solution.py:275
  17.0 7.2 %copy-start.9 = (bf16[256,256]{1,0:T(8,128)(2,1)S(1)}, bf16[256,256]{1,0:T(8,128)(2,1)}, u32[]{:S(2)}) copy-start(bf16[256,256]{1,0:T(8,128)(2,1)} %constant.2.clone.weave_ref) | copy-start | bytes 393220
  19.7 10.1 %collective-permute-start.2 = (bf16[2,10,96,128]{3,2,1,0:T(8,128)(2,1)S(1)}, bf16[2,10,96,128]{3,2,1,0:T(8,128)(2,1)S(1)}, u32[]{:S(2)}, u32[]{:S(2)}) collective-permute-start(bf16[2,10,96,128]{3,2,1,0:T(8,128)(2,1)S(1)} %get-tuple-element.25.new_ref), channel_id=1, source_target_pairs={{0,16},{16,32},{32,48},{48,64},{64,80},{80,96},{96,112},{1,17},{17... | collective-permute-start | bytes 1474568 | tf_op jit(solution)/shard_map/ppermute | solution.py:280
